TPU v7x, 32 devices: a whole 2x2x4 slice. The times are simulated.
32 devices in a mesh: rows: 8 (over z, y), cols: 4 (over x, core).
Axes of the slice: x: 2, y: 2, z: 4, core: 2. Of those that a mesh axis runs over, the one named last changes fastest.
Arguments:
- gradient: float32 [8192, 29568], P('rows', 'cols'), as said below
- start_block: float32 [29568, 64], P('cols'), may hold values from -0.03125 to 0.03125
- activations: float32 [512, 29568], P('rows', 'cols'), may hold values from -6 to 6
- out_grads: float32 [512, 8192], P('rows', 'cols'), may hold values from -6 to 6
Outputs:
- left_factor: float32 [8192, 64], P('rows')
- right_factor: float32 [29568, 64], P('cols')
- scores: float32 [512], P('rows')
Inputs may be any that keep to these rules, and one draw needn't show every extreme that they name: real-valued gradient entries, of order 29568 ** -0.5.
All inputs are finite; a program needn't handle non-finite values.
Results may differ from a plain program's by a relative error of at most 0.00013.
Values sent between devices are 32-bit elements; how exact they have to be, the bound alone decides.
A program may use at most 128 MiB of HBM per device.

v0:
```python
import jax
import jax.numpy as jnp
from jax import lax
from jax.sharding import PartitionSpec as P

ITERS = 2
HIGH = lax.Precision.HIGHEST


def factor_with(block, gram):
    lower = jnp.linalg.cholesky(gram)
    return (
        lax.linalg.triangular_solve(lower, block, left_side=False, lower=True, transpose_a=True),
        lower,
    )


def inner_gram(block):
    return jnp.dot(block.T, block, precision=HIGH, preferred_element_type=jnp.float32)


def per_device(gradient, start_block, activations, out_grads):
    grad_cols = out_grads.shape[1]
    col_index = lax.axis_index("cols")
    omega = start_block
    for step in range(ITERS):
        ysum = lax.psum(
            jnp.dot(gradient, omega, precision=HIGH, preferred_element_type=jnp.float32), "cols"
        )
        gram = lax.psum(inner_gram(ysum), "rows")
        left, lower_y = factor_with(ysum, gram)
        partial_z = jnp.dot(gradient.T, left, precision=HIGH, preferred_element_type=jnp.float32)
        zsum = lax.psum(partial_z, "rows")
        zgram = lax.psum(inner_gram(zsum), "cols")
        right, lower_z = factor_with(zsum, zgram)
        omega = right
    whole_rows = lax.all_gather(left, "rows", axis=0, tiled=True)
    left_cols = lax.dynamic_slice_in_dim(whole_rows, col_index * grad_cols, grad_cols, 0)
    left_part = jnp.dot(out_grads, left_cols, precision=HIGH, preferred_element_type=jnp.float32)
    right_part = jnp.dot(activations, right, precision=HIGH, preferred_element_type=jnp.float32)
    token_left, token_right = lax.psum((left_part, right_part), "cols")
    mixed = jnp.dot(token_left, lower_z, precision=HIGH, preferred_element_type=jnp.float32)
    scores = jnp.sum(mixed * token_right, axis=1)
    return (left, right, scores)


def solution(mesh):
    placed = (P("rows", "cols"), P("cols", None), P("rows", "cols"), P("rows", "cols"))
    return jax.shard_map(
        per_device,
        mesh=mesh,
        in_specs=placed,
        out_specs=(P("rows", None), P("cols", None), P("rows")),
        check_vma=False,
    )
```

profile of v0, /device:TPU:0, one launch (start us, length us, event | category | flops | bytes accessed | tf_op | source)
XLA Modules:
  0.0 579.3 jit_solution(6776016720726716855)
XLA Ops:
  8.7 24.2 %fusion.23 = f32[1024,64]{0,1:T(8,128)} fusion(f32[1024,7392]{0,1:T(8,128)} %param.9, f32[7392,64]{0,1:T(8,128)S(1)} %copy-done), kind=kOutput, calls=%fused_computation.50 | convolution fusion | flops 5813305344 | bytes 32432128 | tf_op jit(solution)/shard_map/dot_general | solution.py:28
  33.0 35.1 %all-reduce.6.cloned.1.call-done = f32[1024,64]{0,1:T(8,128)} async-done(((f32[1024,64]{0,1:T(8,128)}), f32[1024,64]{0,1:T(8,128)}) %all-reduce.6.cloned.1.call-update) | async-done | bytes 262160 | tf_op jit(solution)/shard_map/psum | solution.py:27
  69.5 37.5 %psum.71 = f32[64,64]{0,1:T(8,128)S(1)} all-reduce(f32[64,64]{0,1:T(8,128)S(1)} %fusion.24), channel_id=1, replica_groups=mesh['rows'=8,'cols'=4] {'rows'}, use_global_device_ids=true, to_apply=%region_1.0 | all-reduce | flops 4096 | bytes 32768 | tf_op jit(solution)/shard_map/psum | solution.py:30
  107.1 5.8 %cholesky.74 = f32[64,64]{1,0:T(8,128)S(1)} custom-call(f32[64,64]{1,0:T(8,128)S(1)} %fusion.12), custom_call_target="Cholesky" | custom-call | tf_op jit(solution)/shard_map/jit(cholesky)/cholesky | solution.py:11
  114.3 4.9 custom-call.10
  120.6 30.9 %convolution_bitcast_fusion.3 = f32[7392,64]{0,1:T(8,128)} fusion(f32[1024,64]{0,1:T(8,128)S(1)} %convolution_bitcast_fusion.5, f32[1024,7392]{0,1:T(8,128)} %param.9), kind=kOutput, calls=%fused_computation.3 | convolution fusion | flops 5813305344 | bytes 32432128 | tf_op jit(solution)/shard_map/dot_general | solution.py:32
  151.5 93.6 %all-reduce.8.cloned.1.call-done = f32[7392,64]{0,1:T(8,128)} async-done(((f32[7392,64]{0,1:T(8,128)}), f32[7392,64]{0,1:T(8,128)}) %all-reduce.8.cloned.1.call-update) | async-done | bytes 1892368 | tf_op jit(solution)/shard_map/psum | solution.py:33
  245.1 3.8 fusion.25
  248.9 11.9 %psum.73 = f32[64,64]{0,1:T(8,128)S(1)} all-reduce(f32[64,64]{0,1:T(8,128)S(1)} %fusion.25), channel_id=1, replica_groups=mesh['rows'=8,'cols'=4] {'cols'}, use_global_device_ids=true, to_apply=%region_5.8 | all-reduce | flops 4096 | bytes 32768 | tf_op jit(solution)/shard_map/psum | solution.py:34
  260.9 5.8 %cholesky.85 = f32[64,64]{1,0:T(8,128)S(1)} custom-call(f32[64,64]{1,0:T(8,128)S(1)} %fusion.10), custom_call_target="Cholesky" | custom-call | tf_op jit(solution)/shard_map/jit(cholesky)/cholesky | solution.py:11
  268.1 4.9 custom-call.11
  276.2 23.1 %convolution_bitcast_fusion.6 = f32[1024,64]{0,1:T(8,128)} fusion(f32[7392,64]{0,1:T(8,128)S(1)} %convolution_bitcast_fusion.2, f32[1024,7392]{0,1:T(8,128)} %param.9), kind=kOutput, calls=%fused_computation.6 | convolution fusion | flops 5813305344 | bytes 32432128 | tf_op jit(solution)/shard_map/dot_general | solution.py:28
  299.4 31.0 %all-reduce.10.cloned.1.call-done = f32[1024,64]{0,1:T(8,128)} async-done(((f32[1024,64]{0,1:T(8,128)}), f32[1024,64]{0,1:T(8,128)}) %all-reduce.10.cloned.1.call-update) | async-done | bytes 262160 | tf_op jit(solution)/shard_map/psum | solution.py:27
  331.9 37.4 %psum.75 = f32[64,64]{0,1:T(8,128)S(1)} all-reduce(f32[64,64]{0,1:T(8,128)S(1)} %fusion.26), channel_id=1, replica_groups=mesh['rows'=8,'cols'=4] {'rows'}, use_global_device_ids=true, to_apply=%region_7.11 | all-reduce | flops 4096 | bytes 32768 | tf_op jit(solution)/shard_map/psum | solution.py:30
  369.4 5.8 %cholesky.96 = f32[64,64]{1,0:T(8,128)S(1)} custom-call(f32[64,64]{1,0:T(8,128)S(1)} %fusion.8), custom_call_target="Cholesky" | custom-call | tf_op jit(solution)/shard_map/jit(cholesky)/cholesky | solution.py:11
  376.6 4.9 custom-call.12
  382.9 31.0 %convolution_bitcast_fusion.1 = f32[7392,64]{0,1:T(8,128)} fusion(f32[1024,64]{0,1:T(8,128)S(1)} %convolution_bitcast_fusion.4, f32[1024,7392]{0,1:T(8,128)} %param.9), kind=kOutput, calls=%fused_computation.1 | convolution fusion | flops 5813305344 | bytes 32432128 | tf_op jit(solution)/shard_map/dot_general | solution.py:32
  414.5 93.0 %all-reduce.12.cloned.1.call-done = f32[7392,64]{0,1:T(8,128)} async-done(((f32[7392,64]{0,1:T(8,128)}), f32[7392,64]{0,1:T(8,128)}) %all-reduce.12.cloned.1.call-update) | async-done | bytes 1892368 | tf_op jit(solution)/shard_map/psum | solution.py:33
  507.4 3.8 fusion.27
  511.2 11.6 %psum.77 = f32[64,64]{0,1:T(8,128)S(1)} all-reduce(f32[64,64]{0,1:T(8,128)S(1)} %fusion.27), channel_id=1, replica_groups=mesh['rows'=8,'cols'=4] {'cols'}, use_global_device_ids=true, to_apply=%region_9.13 | all-reduce | flops 4096 | bytes 32768 | tf_op jit(solution)/shard_map/psum | solution.py:34
  522.9 5.8 %cholesky.107 = f32[64,64]{1,0:T(8,128)S(1)} custom-call(f32[64,64]{1,0:T(8,128)S(1)} %fusion.6), custom_call_target="Cholesky" | custom-call | tf_op jit(solution)/shard_map/jit(cholesky)/cholesky | solution.py:11
  530.0 4.9 custom-call.13
  541.3 17.6 %all-gather.2.cloned.1.call-done = f32[8192,64]{0,1:T(8,128)} async-done(((f32[1024,64]{0,1:T(8,128)}), f32[8192,64]{0,1:T(8,128)}) %all-gather.2.cloned.1.call-update) | async-done | bytes 2097168 | tf_op jit(solution)/shard_map/all_gather | solution.py:37
  560.5 10.7 %all-reduce = (f32[64,64]{0,1:T(8,128)S(1)}, f32[64,64]{0,1:T(8,128)S(1)}) all-reduce(f32[64,64]{0,1:T(8,128)S(1)} %convolution_bitcast_fusion.7, f32[64,64]{0,1:T(8,128)S(1)} %convolution_bitcast_fusion.8), channel_id=1, replica_groups=mesh['rows'=8,'cols'=4] {'cols'}, use_global_device_ids=true, to_apply=%region_11.15 | all-reduce | flops 8192 | bytes 65536 | tf_op jit(solution)/shard_map/psum | solution.py:41
  (49 shorter events, 25.9 us)
Async XLA Ops:
  7.2 1.5 copy-start
  7.2 60.9 %all-reduce.6.cloned.1.call-start = ((), (), s32[]{:S(2)}) async-start(), calls=%async_computation | async-start | bytes 524288 | tf_op jit(solution)/shard_map/psum | solution.py:27
  32.9 212.2 %all-reduce.8.cloned.1.call-start = ((), (), s32[]{:S(2)}) async-start(), calls=%async_computation.1 | async-start | bytes 3801088 | tf_op jit(solution)/shard_map/psum | solution.py:33
  151.5 179.0 %all-reduce.10.cloned.1.call-start = ((), (), s32[]{:S(2)}) async-start(), calls=%async_computation.2 | async-start | bytes 524288 | tf_op jit(solution)/shard_map/psum | solution.py:27
  299.4 208.0 %all-reduce.12.cloned.1.call-start = ((), (), s32[]{:S(2)}) async-start(), calls=%async_computation.3 | async-start | bytes 3801088 | tf_op jit(solution)/shard_map/psum | solution.py:33
  382.8 31.0 %copy-start.2 = (f32[1024,64]{0,1:T(8,128)}, f32[1024,64]{0,1:T(8,128)S(1)}, u32[]{:S(2)}) copy-start(f32[1024,64]{0,1:T(8,128)S(1)} %convolution_bitcast_fusion.4) | copy-start | bytes 786436
  413.9 145.0 %all-gather.2.cloned.1.call-start = ((), (), s32[]{:S(2)}) async-start(), calls=%async_computation.4 | async-start | bytes 2359296 | tf_op jit(solution)/shard_map/all_gather | solution.py:37
  534.9 4.7 copy-start.3
  538.3 1.3 copy-start.1
  539.6 19.3 %copy-start.4 = (f32[64,2048]{1,0:T(8,128)S(1)}, f32[64,2048]{1,0:T(8,128)}, u32[]{:S(2)}) copy-start(f32[64,2048]{1,0:T(8,128)} %param.12) | copy-start | bytes 1572868
Sparse Core Ops, SparseCore 0:
  33.0 35.0 all-reduce.5
  151.6 93.4 all-reduce.7
  299.5 30.9 all-reduce.9
  414.0 93.4 all-reduce.11
  510.1 48.7 all-gather.1
where the time goes:
time: 583 us; the launch traced here: 579 us
  waiting for transfers between devices  271 us (46%)
  matrix products  133 us (23%)
  blocking collectives  109 us (19%)
  other arithmetic  48.2 us (8%)
  between operations  14.2 us (2%)
    psum x2, waiting for transfers between devices, per_device(): zsum = lax.psum(partial_z, 'rows')  187 us
    psum x2, blocking collectives, per_device(): gram = lax.psum(inner_gram(ysum), 'rows')  74.9 us
    psum x2, waiting for transfers between devices, per_device(): lax.psum(jnp.dot(gradient, omega, precision=HIGH, preferred_element_type=...  66.2 us
    dot_general x2, matrix products, per_device(): jnp.dot(gradient.T, left, precision=HIGH, preferred_element_type=jnp.floa...  61.9 us
    dot_general x2, matrix products, per_device(): jnp.dot(gradient, omega, precision=HIGH, preferred_element_type=jnp.float32)  47.3 us
    another operation x12, other arithmetic, factor_with(): lower = jnp.linalg.cholesky(gram)  26.1 us
    psum x2, blocking collectives, per_device(): zgram = lax.psum(inner_gram(zsum), 'cols')  23.5 us
    another operation x8, other arithmetic, factor_with(): lax.linalg.triangular_solve(lower, block, left_side=False, lower=True, tr...  22.1 us
  transfers between devices with their start and end apart: 5, of which 5 were waited for; matrix products, arithmetic and copies ran while one was open for 4% of the time, Pallas kernels for 0%

commit v1 on v0

--- a/solution.py
+++ b/solution.py
@@ -5,6 +5,14 @@
 
 ITERS = 2
 HIGH = lax.Precision.HIGHEST
+
+
+def doubling_sum(x, mesh_axis):
+    peers, total = (lax.axis_size(mesh_axis), x)
+    for hop in [1 << k for k in range(peers.bit_length() - 1)]:
+        swap = [(i, i ^ hop) for i in range(peers)]
+        total = total + lax.ppermute(total, mesh_axis, swap)
+    return total
 
 
 def factor_with(block, gram):
@@ -30,7 +38,7 @@
         gram = lax.psum(inner_gram(ysum), "rows")
         left, lower_y = factor_with(ysum, gram)
         partial_z = jnp.dot(gradient.T, left, precision=HIGH, preferred_element_type=jnp.float32)
-        zsum = lax.psum(partial_z, "rows")
+        zsum = doubling_sum(partial_z, "rows")
         zgram = lax.psum(inner_gram(zsum), "cols")
         right, lower_z = factor_with(zsum, zgram)
         omega = right

time: 583 us -> 679 us (1.16)
  waiting for transfers between devices: 271 us -> 369 us
  matrix products: 133 us -> 126 us
    ppermute x0 -> x6, waiting for transfers between devices: none -> 303 us  [doubling_sum(): total = total + lax.ppermute(total, mesh_axis, swap)]
    psum x2 -> x0, waiting for transfers between devices: 187 us -> none  [per_device(): zsum = lax.psum(partial_z, 'rows')]
    all_gather x1, waiting for transfers between devices: 17.6 us -> 0.02 us  [per_device(): whole_rows = lax.all_gather(left, 'rows', axis=0, tiled=True)]
  transfers between devices with their start and end apart: 5 -> 9, of which waited for: 5 -> 8; matrix products, arithmetic and copies ran while one was open for 4% -> 1% of each run, Pallas kernels for 0% -> 0%
where the time goes in v1:
time: 679 us; the launch traced here: 675 us
  waiting for transfers between devices  369 us (54%)
  matrix products  126 us (19%)
  blocking collectives  109 us (16%)
  other arithmetic  53.3 us (8%)
  between operations  14.4 us (2%)
    ppermute x6, waiting for transfers between devices, doubling_sum(): total = total + lax.ppermute(total, mesh_axis, swap)  303 us
    psum x2, blocking collectives, per_device(): gram = lax.psum(inner_gram(ysum), 'rows')  74.9 us
    psum x2, waiting for transfers between devices, per_device(): lax.psum(jnp.dot(gradient, omega, precision=HIGH, preferred_element_type=...  65.8 us
    dot_general x2, matrix products, per_device(): jnp.dot(gradient.T, left, precision=HIGH, preferred_element_type=jnp.floa...  59.6 us
    dot_general x2, matrix products, per_device(): jnp.dot(gradient, omega, precision=HIGH, preferred_element_type=jnp.float32)  47.3 us
    another operation x12, other arithmetic, factor_with(): lower = jnp.linalg.cholesky(gram)  26.2 us
    another operation x8, other arithmetic, factor_with(): lax.linalg.triangular_solve(lower, block, left_side=False, lower=True, tr...  22.2 us
    psum x2, blocking collectives, per_device(): zgram = lax.psum(inner_gram(zsum), 'cols')  21.9 us
  transfers between devices with their start and end apart: 9, of which 8 were waited for; matrix products, arithmetic and copies ran while one was open for 1% of the time, Pallas kernels for 0%

profile of v1, /device:TPU:0, one launch (start us, length us, event | category | flops | bytes accessed | tf_op | source)
XLA Modules:
  0.0 675.3 jit_solution(4455810772178750433)
XLA Ops:
  8.7 24.2 %fusion.23 = f32[1024,64]{0,1:T(8,128)} fusion(f32[1024,7392]{0,1:T(8,128)} %param.9, f32[7392,64]{0,1:T(8,128)S(1)} %copy-done), kind=kOutput, calls=%fused_computation.50 | convolution fusion | flops 5813305344 | bytes 32432128 | tf_op jit(solution)/shard_map/dot_general | solution.py:36
  33.0 35.1 %all-reduce.4.cloned.1.call-done = f32[1024,64]{0,1:T(8,128)} async-done(((f32[1024,64]{0,1:T(8,128)}), f32[1024,64]{0,1:T(8,128)}) %all-reduce.4.cloned.1.call-update) | async-done | bytes 262160 | tf_op jit(solution)/shard_map/psum | solution.py:35
  69.5 37.5 %psum.57 = f32[64,64]{0,1:T(8,128)S(1)} all-reduce(f32[64,64]{0,1:T(8,128)S(1)} %fusion.24), channel_id=1, replica_groups=mesh['rows'=8,'cols'=4] {'rows'}, use_global_device_ids=true, to_apply=%region_1.0 | all-reduce | flops 4096 | bytes 32768 | tf_op jit(solution)/shard_map/psum | solution.py:38
  107.1 5.8 cholesky.74
  114.2 4.9 custom-call.10
  120.5 29.8 %convolution_bitcast_fusion.3 = f32[7392,64]{0,1:T(8,128)S(1)} fusion(f32[1024,64]{0,1:T(8,128)S(1)} %convolution_bitcast_fusion.5, f32[1024,7392]{0,1:T(8,128)} %param.9), kind=kOutput, calls=%fused_computation.3 | convolution fusion | flops 5813305344 | bytes 32432128 | tf_op jit(solution)/shard_map/dot_general | solution.py:40
  150.4 34.7 %collective-permute-done = f32[7392,64]{0,1:T(8,128)S(1)} collective-permute-done((f32[7392,64]{0,1:T(8,128)S(1)}, f32[7392,64]{0,1:T(8,128)S(1)}, u32[]{:S(2)}, u32[]{:S(2)}) %collective-permute-start) | collective-permute-done | bytes 1892384 | tf_op jit(solution)/shard_map/ppermute | solution.py:14
  185.4 38.9 %collective-permute-done.1 = f32[7392,64]{0,1:T(8,128)S(1)} collective-permute-done((f32[7392,64]{0,1:T(8,128)S(1)}, f32[7392,64]{0,1:T(8,128)S(1)}, u32[]{:S(2)}, u32[]{:S(2)}) %collective-permute-start.1) | collective-permute-done | bytes 1892384 | tf_op jit(solution)/shard_map/ppermute | solution.py:14
  224.8 69.6 %collective-permute-done.2 = f32[7392,64]{0,1:T(8,128)S(1)} collective-permute-done((f32[7392,64]{0,1:T(8,128)S(1)}, f32[7392,64]{0,1:T(8,128)S(1)}, u32[]{:S(2)}, u32[]{:S(2)}) %collective-permute-start.2) | collective-permute-done | bytes 1892384 | tf_op jit(solution)/shard_map/ppermute | solution.py:14
  296.3 11.4 %psum.58 = f32[64,64]{0,1:T(8,128)S(1)} all-reduce(f32[64,64]{0,1:T(8,128)S(1)} %fusion.25), channel_id=1, replica_groups=mesh['rows'=8,'cols'=4] {'cols'}, use_global_device_ids=true, to_apply=%region_4.7 | all-reduce | flops 4096 | bytes 32768 | tf_op jit(solution)/shard_map/psum | solution.py:42
  307.8 5.8 cholesky.85
  315.0 4.9 custom-call.11
  321.7 23.1 %convolution_bitcast_fusion.6 = f32[1024,64]{0,1:T(8,128)} fusion(f32[7392,64]{0,1:T(8,128)S(1)} %convolution_bitcast_fusion.2, f32[1024,7392]{0,1:T(8,128)} %param.9), kind=kOutput, calls=%fused_computation.6 | convolution fusion | flops 5813305344 | bytes 32432128 | tf_op jit(solution)/shard_map/dot_general | solution.py:36
  344.9 30.7 %all-reduce.6.cloned.1.call-done = f32[1024,64]{0,1:T(8,128)} async-done(((f32[1024,64]{0,1:T(8,128)}), f32[1024,64]{0,1:T(8,128)}) %all-reduce.6.cloned.1.call-update) | async-done | bytes 262160 | tf_op jit(solution)/shard_map/psum | solution.py:35
  376.9 37.4 %psum.60 = f32[64,64]{0,1:T(8,128)S(1)} all-reduce(f32[64,64]{0,1:T(8,128)S(1)} %fusion.26), channel_id=1, replica_groups=mesh['rows'=8,'cols'=4] {'rows'}, use_global_device_ids=true, to_apply=%region_6.10 | all-reduce | flops 4096 | bytes 32768 | tf_op jit(solution)/shard_map/psum | solution.py:38
  414.4 5.8 cholesky.96
  427.9 29.7 %convolution_bitcast_fusion.1 = f32[7392,64]{0,1:T(8,128)S(1)} fusion(f32[1024,64]{0,1:T(8,128)S(1)} %convolution_bitcast_fusion.4, f32[1024,7392]{0,1:T(8,128)} %param.9), kind=kOutput, calls=%fused_computation.1 | convolution fusion | flops 5813305344 | bytes 32432128 | tf_op jit(solution)/shard_map/dot_general | solution.py:40
  457.7 48.9 %collective-permute-done.3 = f32[7392,64]{0,1:T(8,128)} collective-permute-done((f32[7392,64]{0,1:T(8,128)S(1)}, f32[7392,64]{0,1:T(8,128)}, u32[]{:S(2)}, u32[]{:S(2)}) %collective-permute-start.3) | collective-permute-done | bytes 1892384 | tf_op jit(solution)/shard_map/ppermute | solution.py:14
  508.4 41.3 %collective-permute-done.4 = f32[7392,64]{0,1:T(8,128)S(1)} collective-permute-done((f32[7392,64]{0,1:T(8,128)S(1)}, f32[7392,64]{0,1:T(8,128)S(1)}, u32[]{:S(2)}, u32[]{:S(2)}) %collective-permute-start.4) | collective-permute-done | bytes 1892384 | tf_op jit(solution)/shard_map/ppermute | solution.py:14
  552.1 69.4 %collective-permute-done.5 = f32[7392,64]{0,1:T(8,128)} collective-permute-done((f32[7392,64]{0,1:T(8,128)S(1)}, f32[7392,64]{0,1:T(8,128)}, u32[]{:S(2)}, u32[]{:S(2)}) %collective-permute-start.5) | collective-permute-done | bytes 1892384 | tf_op jit(solution)/shard_map/ppermute | solution.py:14
  625.5 10.5 %psum.61 = f32[64,64]{0,1:T(8,128)S(1)} all-reduce(f32[64,64]{0,1:T(8,128)S(1)} %fusion.27), channel_id=1, replica_groups=mesh['rows'=8,'cols'=4] {'cols'}, use_global_device_ids=true, to_apply=%region_7.11 | all-reduce | flops 4096 | bytes 32768 | tf_op jit(solution)/shard_map/psum | solution.py:42
  636.0 5.8 cholesky.107
  643.3 4.9 custom-call.13
  654.6 12.5 %all-reduce = (f32[64,64]{0,1:T(8,128)S(1)}, f32[64,64]{0,1:T(8,128)S(1)}) all-reduce(f32[64,64]{0,1:T(8,128)S(1)} %convolution_bitcast_fusion.7, f32[64,64]{0,1:T(8,128)S(1)} %convolution_bitcast_fusion.8), channel_id=1, replica_groups=mesh['rows'=8,'cols'=4] {'cols'}, use_global_device_ids=true, to_apply=%region_9.13 | all-reduce | flops 8192 | bytes 65536 | tf_op jit(solution)/shard_map/psum | solution.py:49
  (67 shorter events, 38.0 us)
Async XLA Ops:
  7.2 1.5 copy-start
  7.2 60.9 %all-reduce.4.cloned.1.call-start = ((), (), s32[]{:S(2)}) async-start(), calls=%async_computation | async-start | bytes 524288 | tf_op jit(solution)/shard_map/psum | solution.py:35
  32.9 342.6 %all-reduce.6.cloned.1.call-start = ((), (), s32[]{:S(2)}) async-start(), calls=%async_computation.1 | async-start | bytes 524288 | tf_op jit(solution)/shard_map/psum | solution.py:35
  150.4 34.8 %collective-permute-start = (f32[7392,64]{0,1:T(8,128)S(1)}, f32[7392,64]{0,1:T(8,128)S(1)}, u32[]{:S(2)}, u32[]{:S(2)}) collective-permute-start(f32[7392,64]{0,1:T(8,128)S(1)} %convolution_bitcast_fusion.3), channel_id=1, source_target_pairs={{0,4},{4,0},{8,12},{12,8},{16,20},{20,16},{24,28},{28,24},{1,5},{5... | collective-permute-start | bytes 5677064 | tf_op jit(solution)/shard_map/ppermute | solution.py:14
  185.4 39.0 %collective-permute-start.1 = (f32[7392,64]{0,1:T(8,128)S(1)}, f32[7392,64]{0,1:T(8,128)S(1)}, u32[]{:S(2)}, u32[]{:S(2)}) collective-permute-start(f32[7392,64]{0,1:T(8,128)S(1)} %add.46), channel_id=1, source_target_pairs={{0,8},{4,12},{8,0},{12,4},{16,24},{20,28},{24,16},{28,20},{1,9},{5... | collective-permute-start | bytes 5677064 | tf_op jit(solution)/shard_map/ppermute | solution.py:14
  224.8 69.7 %collective-permute-start.2 = (f32[7392,64]{0,1:T(8,128)S(1)}, f32[7392,64]{0,1:T(8,128)S(1)}, u32[]{:S(2)}, u32[]{:S(2)}) collective-permute-start(f32[7392,64]{0,1:T(8,128)S(1)} %add.47), channel_id=1, source_target_pairs={{0,16},{4,20},{8,24},{12,28},{16,0},{20,4},{24,8},{28,12},{1,17},{... | collective-permute-start | bytes 5677064 | tf_op jit(solution)/shard_map/ppermute | solution.py:14
  344.8 205.3 %all-gather.2.cloned.1.call-start = ((), (), s32[]{:S(2)}) async-start(), calls=%async_computation.2 | async-start | bytes 2359296 | tf_op jit(solution)/shard_map/all_gather | solution.py:45
  427.9 29.8 %copy-start.5 = (f32[1024,64]{0,1:T(8,128)}, f32[1024,64]{0,1:T(8,128)S(1)}, u32[]{:S(2)}) copy-start(f32[1024,64]{0,1:T(8,128)S(1)} %convolution_bitcast_fusion.4) | copy-start | bytes 786436
  457.6 49.0 %collective-permute-start.3 = (f32[7392,64]{0,1:T(8,128)S(1)}, f32[7392,64]{0,1:T(8,128)}, u32[]{:S(2)}, u32[]{:S(2)}) collective-permute-start(f32[7392,64]{0,1:T(8,128)S(1)} %convolution_bitcast_fusion.1), channel_id=1, source_target_pairs={{0,4},{4,0},{8,12},{12,8},{16,20},{20,16},{24,28},{28,24},{1,5},{5... | collective-permute-start | bytes 5677064 | tf_op jit(solution)/shard_map/ppermute | solution.py:14
  508.3 41.8 %copy-start.7 = (f32[64,2048]{1,0:T(8,128)S(1)}, f32[64,2048]{1,0:T(8,128)}, u32[]{:S(2)}) copy-start(f32[64,2048]{1,0:T(8,128)} %param.12) | copy-start | bytes 1572868
  508.3 41.4 %collective-permute-start.4 = (f32[7392,64]{0,1:T(8,128)S(1)}, f32[7392,64]{0,1:T(8,128)S(1)}, u32[]{:S(2)}, u32[]{:S(2)}) collective-permute-start(f32[7392,64]{0,1:T(8,128)S(1)} %add.49), channel_id=1, source_target_pairs={{0,8},{4,12},{8,0},{12,4},{16,24},{20,28},{24,16},{28,20},{1,9},{5... | collective-permute-start | bytes 5677064 | tf_op jit(solution)/shard_map/ppermute | solution.py:14
  550.0 2.1 copy-start.3
  550.0 71.5 %collective-permute-start.5 = (f32[7392,64]{0,1:T(8,128)S(1)}, f32[7392,64]{0,1:T(8,128)}, u32[]{:S(2)}, u32[]{:S(2)}) collective-permute-start(f32[7392,64]{0,1:T(8,128)S(1)} %add.50), channel_id=1, source_target_pairs={{0,16},{4,20},{8,24},{12,28},{16,0},{20,4},{24,8},{28,12},{1,17},{... | collective-permute-start | bytes 5677064 | tf_op jit(solution)/shard_map/ppermute | solution.py:14
  623.8 1.6 copy-start.2
  648.2 4.7 copy-start.6
  648.3 20.3 %copy-start.1 = (f32[7392,64]{0,1:T(8,128)S(1)}, f32[7392,64]{0,1:T(8,128)}, u32[]{:S(2)}) copy-start(f32[7392,64]{0,1:T(8,128)} %param.10) | copy-start | bytes 5677060
  651.7 1.3 copy-start.4
Sparse Core Ops, SparseCore 0:
  33.0 34.9 all-reduce.3
  344.9 30.5 all-reduce.5
  457.9 56.8 all-gather.1
